TPU v7x, 32 devices: a whole 2x2x4 slice. The times are simulated.
32 devices in a mesh: layer: 4 (over z), row: 2 (over core), col: 4 (over y, x).
Axes of the slice: x: 2, y: 2, z: 4, core: 2. Of those that a mesh axis runs over, the one named last changes fastest.
Arguments:
- panels: float32 [4096, 8192], P('row', ('layer', 'col')), may hold values from -0.0625 to 0.0625
- eigvecs: float32 [8192, 2048], P(('layer', 'row'), 'col'), may hold values from -6 to 6
Outputs:
- result: float32 [4096, 2048], P('row', 'col')
All inputs are finite; a program needn't handle non-finite values.
Results may differ from a plain program's by a relative error of at most 0.0001.
Values sent between devices are 32-bit elements; how exact they have to be, the bound alone decides.
No kernel may reach another device: no remote copies, remote signals or barrier semaphores. Data moves between devices by JAX's collectives and lax.ppermute only.
A program may use at most 64 MiB of HBM per device.

v0:
```python
import jax
import jax.numpy as jnp
from jax import lax
from jax.sharding import PartitionSpec as P


def local(panels, eigvecs):
    layer_vecs = lax.all_gather(eigvecs, "row", axis=0, tiled=True)
    partial_sum = jnp.dot(
        lax.all_gather(panels, "col", axis=1, tiled=True),
        layer_vecs,
        preferred_element_type=jnp.float32,
        precision=lax.Precision.HIGHEST,
    )
    result = lax.psum(partial_sum, "layer")
    return result


def solution(mesh):
    in_specs = (P("row", ("layer", "col")), P(("layer", "row"), "col"))
    out_specs = P("row", "col")
    return jax.shard_map(local, mesh=mesh, in_specs=in_specs, out_specs=out_specs, check_vma=False)
```

profile of v0, /device:TPU:0, one launch (start us, length us, event | category | flops | bytes accessed | tf_op | source)
XLA Modules:
  0.0 383.9 jit_solution(4425001586556484213)
XLA Ops:
  6.5 0.0 all-gather.5.cloned.1.call-start
  6.5 0.7 all-gather.5.cloned.1.call-update
  7.3 0.0 all-gather.3.cloned.1.call-start
  7.3 0.7 all-gather.3.cloned.1.call-update
  8.0 0.0 all-reduce.2.cloned.1.call-start
  8.1 17.2 %all-gather.5.cloned.1.call-done = f32[2048,512]{1,0:T(8,128)} async-done(((f32[1024,512]{1,0:T(8,128)}), f32[2048,512]{1,0:T(8,128)}) %all-gather.5.cloned.1.call-update) | async-done | bytes 4194320 | tf_op jit(solution)/shard_map/all_gather | solution.py:8
  25.3 160.3 %all-gather.3.cloned.1.call-done = f32[2048,2048]{1,0:T(8,128)} async-done(((f32[2048,512]{1,0:T(8,128)}), f32[2048,2048]{1,0:T(8,128)}) %all-gather.3.cloned.1.call-update) | async-done | bytes 16777232 | tf_op jit(solution)/shard_map/all_gather | solution.py:10
  185.6 31.9 %fusion = f32[2048,512]{1,0:T(8,128)} fusion(f32[2048,2048]{1,0:T(8,128)} %all-gather.3.cloned.1.call-done, f32[2048,512]{1,0:T(8,128)} %all-gather.5.cloned.1.call-done), kind=kOutput, calls=%fused_computation | convolution fusion | flops 25769803776 | bytes 25165824 | tf_op jit(solution)/shard_map/dot_general | solution.py:9
  217.6 0.0 all-reduce.2.cloned.1.call-update
  217.6 155.1 %all-reduce.2.cloned.1.call-done = f32[2048,512]{1,0:T(8,128)} async-done(((f32[2048,512]{1,0:T(8,128)}), f32[2048,512]{1,0:T(8,128)}) %all-reduce.2.cloned.1.call-update) | async-done | bytes 4194320 | tf_op jit(solution)/shard_map/psum | solution.py:15
  372.7 4.6 %copy.4 = f32[2048,512]{1,0:T(8,128)} copy(f32[2048,512]{1,0:T(8,128)} %all-reduce.2.cloned.1.call-done) | data formatting | bytes 8388608
Async XLA Ops:
  6.5 18.8 %all-gather.5.cloned.1.call-start = ((), (), s32[]{:S(2)}) async-start(), calls=%async_computation.1 | async-start | bytes 6291456 | tf_op jit(solution)/shard_map/all_gather | solution.py:8
  7.3 178.4 %all-gather.3.cloned.1.call-start = ((), (), s32[]{:S(2)}) async-start(), calls=%async_computation | async-start | bytes 20971520 | tf_op jit(solution)/shard_map/all_gather | solution.py:10
  8.0 364.7 %all-reduce.2.cloned.1.call-start = ((), (), s32[]{:S(2)}) async-start(), calls=%async_computation.2 | async-start | bytes 8388608 | tf_op jit(solution)/shard_map/psum | solution.py:15
Sparse Core Ops, SparseCore 0:
  8.9 16.3 all-gather.4
  27.1 158.4 all-gather.2
  217.7 154.9 all-reduce.1
where the time goes:
time: 384 us
  waiting for transfers between devices  334 us (87%)
  matrix products  31.9 us (8%)
  between operations  13.1 us (3%)
  local copies, waits for them, and re-layouts  4.64 us (1%)
    all_gather x1, waiting for transfers between devices, local(): lax.all_gather(panels, 'col', axis=1, tiled=True)  160 us
    psum x1, waiting for transfers between devices, local(): result = lax.psum(partial_sum, 'layer')  155 us
    dot_general x1, matrix products, local(): jnp.dot(lax.all_gather(panels, 'col', axis=1, tiled=True), layer_vecs, pr...  31.9 us
    all_gather x1, waiting for transfers between devices, local(): layer_vecs = lax.all_gather(eigvecs, 'row', axis=0, tiled=True)  17.2 us
  transfers between devices with their start and end apart: 3, of which 3 were waited for; matrix products, arithmetic and copies ran while one was open for 0% of the time, Pallas kernels for 0%

commit v1 on v0

--- a/solution.py
+++ b/solution.py
@@ -12,7 +12,9 @@
         preferred_element_type=jnp.float32,
         precision=lax.Precision.HIGHEST,
     )
-    result = lax.psum(partial_sum, "layer")
+    result = partial_sum
+    for hop in (1, 2):
+        result = result + lax.ppermute(result, "layer", [(dev, dev ^ hop) for dev in range(4)])
     return result
 
 

time: 384 us -> 503 us (1.31)
  waiting for transfers between devices: 334 us -> 449 us
    ppermute x0 -> x2, waiting for transfers between devices: none -> 270 us  [local(): lax.ppermute(result, 'layer', [(dev, dev ^ hop) for dev in range(4)])]
    psum x1 -> x0, waiting for transfers between devices: 155 us -> none  [local(): result = lax.psum(partial_sum, 'layer')]
  transfers between devices with their start and end apart: 3 -> 4, of which waited for: 3 -> 4; matrix products, arithmetic and copies ran while one was open for 0% -> 0% of each run, Pallas kernels for 0% -> 0%
where the time goes in v1:
time: 503 us
  waiting for transfers between devices  449 us (89%)
  matrix products  32 us (6%)
  between operations  13.4 us (3%)
    ppermute x2, waiting for transfers between devices, local(): lax.ppermute(result, 'layer', [(dev, dev ^ hop) for dev in range(4)])  270 us
    all_gather x1, waiting for transfers between devices, local(): lax.all_gather(panels, 'col', axis=1, tiled=True)  160 us
    dot_general x1, matrix products, local(): jnp.dot(lax.all_gather(panels, 'col', axis=1, tiled=True), layer_vecs, pr...  32 us
    all_gather x1, waiting for transfers between devices, local(): layer_vecs = lax.all_gather(eigvecs, 'row', axis=0, tiled=True)  17.3 us
  transfers between devices with their start and end apart: 4, of which 4 were waited for; matrix products, arithmetic and copies ran while one was open for 0% of the time, Pallas kernels for 0%

profile of v1, /device:TPU:0, one launch (start us, length us, event | category | flops | bytes accessed | tf_op | source)
XLA Modules:
  0.0 502.9 jit_solution(4564204904647918365)
XLA Ops:
  6.5 0.0 all-gather.5.cloned.1.call-start
  6.5 0.7 all-gather.5.cloned.1.call-update
  7.3 0.0 all-gather.3.cloned.1.call-start
  7.3 0.7 all-gather.3.cloned.1.call-update
  8.0 17.3 %all-gather.5.cloned.1.call-done = f32[2048,512]{1,0:T(8,128)} async-done(((f32[1024,512]{1,0:T(8,128)}), f32[2048,512]{1,0:T(8,128)}) %all-gather.5.cloned.1.call-update) | async-done | bytes 4194320 | tf_op jit(solution)/shard_map/all_gather | solution.py:8
  25.3 160.3 %all-gather.3.cloned.1.call-done = f32[2048,2048]{1,0:T(8,128)} async-done(((f32[2048,512]{1,0:T(8,128)}), f32[2048,2048]{1,0:T(8,128)}) %all-gather.3.cloned.1.call-update) | async-done | bytes 16777232 | tf_op jit(solution)/shard_map/all_gather | solution.py:10
  185.6 32.0 %fusion = f32[2048,512]{1,0:T(8,128)S(1)} fusion(f32[2048,2048]{1,0:T(8,128)} %all-gather.3.cloned.1.call-done, f32[2048,512]{1,0:T(8,128)} %all-gather.5.cloned.1.call-done), kind=kOutput, calls=%fused_computation | convolution fusion | flops 25769803776 | bytes 25165824 | tf_op jit(solution)/shard_map/dot_general | solution.py:9
  217.6 1.6 collective-permute-start
  219.2 90.7 %collective-permute-done = f32[2048,512]{1,0:T(8,128)S(1)} collective-permute-done((f32[2048,512]{1,0:T(8,128)S(1)}, f32[2048,512]{1,0:T(8,128)S(1)}, u32[]{:S(2)}, u32[]{:S(2)}) %collective-permute-start) | collective-permute-done | bytes 4194336 | tf_op jit(solution)/shard_map/ppermute | solution.py:17
  309.9 1.0 add.6
  310.9 2.5 collective-permute-start.1
  313.3 179.7 %collective-permute-done.1 = f32[2048,512]{1,0:T(8,128)S(1)} collective-permute-done((f32[2048,512]{1,0:T(8,128)S(1)}, f32[2048,512]{1,0:T(8,128)S(1)}, u32[]{:S(2)}, u32[]{:S(2)}) %collective-permute-start.1) | collective-permute-done | bytes 4194336 | tf_op jit(solution)/shard_map/ppermute | solution.py:17
  493.0 3.0 add.7
Async XLA Ops:
  6.5 18.8 %all-gather.5.cloned.1.call-start = ((), (), s32[]{:S(2)}) async-start(), calls=%async_computation.1 | async-start | bytes 6291456 | tf_op jit(solution)/shard_map/all_gather | solution.py:8
  7.3 178.4 %all-gather.3.cloned.1.call-start = ((), (), s32[]{:S(2)}) async-start(), calls=%async_computation | async-start | bytes 20971520 | tf_op jit(solution)/shard_map/all_gather | solution.py:10
  217.6 92.2 %collective-permute-start = (f32[2048,512]{1,0:T(8,128)S(1)}, f32[2048,512]{1,0:T(8,128)S(1)}, u32[]{:S(2)}, u32[]{:S(2)}) collective-permute-start(f32[2048,512]{1,0:T(8,128)S(1)} %fusion), channel_id=1, source_target_pairs={{0,8},{8,0},{16,24},{24,16},{1,9},{9,1},{17,25},{25,17},{2,10},{10... | collective-permute-start | bytes 12582920 | tf_op jit(solution)/shard_map/ppermute | solution.py:17
  310.9 182.1 %collective-permute-start.1 = (f32[2048,512]{1,0:T(8,128)S(1)}, f32[2048,512]{1,0:T(8,128)S(1)}, u32[]{:S(2)}, u32[]{:S(2)}) collective-permute-start(f32[2048,512]{1,0:T(8,128)S(1)} %add.6), channel_id=1, source_target_pairs={{0,16},{8,24},{16,0},{24,8},{1,17},{9,25},{17,1},{25,9},{2,18},{10... | collective-permute-start | bytes 12582920 | tf_op jit(solution)/shard_map/ppermute | solution.py:17
Sparse Core Ops, SparseCore 0:
  8.9 16.3 all-gather.4
  27.1 158.4 all-gather.2
